TPU v7x, 32 devices: a whole 2x2x4 slice. The times are simulated.
32 devices in a mesh: gx: 4 (over y, core), gy: 8 (over z, x).
Axes of the slice: x: 2, y: 2, z: 4, core: 2. Of those that a mesh axis runs over, the one named last changes fastest.
Arguments:
- wavefield: float32 [8, 16, 3, 125, 256], P('gx', 'gy'), may hold values from -0.6 to 0.6
- moduli: float32 [8, 16, 2, 256], P('gx', 'gy'), may hold values from 0.5 to 4
- residuals: float32 [32, 32, 128], P(('gx', 'gy')), may hold values from -6 to 6
- coords: float32 [32, 32, 3, 128], P(('gx', 'gy')), may hold values from -1 to 1
- angles: float32 [32, 32, 2, 128], P(('gx', 'gy')), may hold values from -3.140625 to 3.140625
- element_ids: int32 [32, 32, 128], P(('gx', 'gy')), may hold values from 0 to 1023
- counts: int32 [32, 32], P(('gx', 'gy')), may hold values from 0 to 128, as said below
Outputs:
- force: float32 [8, 16, 3, 125, 256], P('gx', 'gy')
Inputs may be any that keep to these rules, and one draw needn't show every extreme that they name: `counts`: each sending device has at least one tile with exactly 128 live slots; in every draw one owner receives 128 live slots from every sender. The lightest owners receive on average about a sixth of 128 a sender, the others lie between.
All inputs are finite; a program needn't handle non-finite values.
Results may differ from a plain program's by a relative error of at most 0.0003.
Values sent between devices are 32-bit elements; how exact they have to be, the bound alone decides.
A program may use at most 64 MiB of HBM per device.

v0:
```python
import math

import jax
import jax.numpy as jnp
import numpy as np
from jax import lax
from jax.sharding import PartitionSpec as P


def with_halo(block, sides, width):
    for axis, dim in sides:
        count = lax.axis_size(axis)
        forward = [(i, i + 1) for i in range(count - 1)]
        backward = [(target, source) for source, target in forward]
        low = lax.ppermute(
            lax.slice_in_dim(block, block.shape[dim] - width, None, axis=dim), axis, forward
        )
        high = lax.ppermute(lax.slice_in_dim(block, 0, width, axis=dim), axis, backward)
        block = jnp.concatenate([low, block, high], axis=dim)
    return block


def gll_points():
    return np.array([-1.0, -math.sqrt(3.0 / 7.0), 0.0, math.sqrt(3.0 / 7.0), 1.0])


def gll_weights():
    return np.array([0.1, 49.0 / 90.0, 32.0 / 45.0, 49.0 / 90.0, 0.1])


def derivative_table():
    points = gll_points()
    table = np.zeros((5, 5))
    for row in range(5):
        for col in range(5):
            if row == col:
                table[row, col] = sum(
                    (1.0 / (points[col] - points[other]) for other in range(5) if other != col)
                )
            else:
                value = 1.0 / (points[col] - points[row])
                for other in range(5):
                    if other != col and other != row:
                        value = (
                            value * (points[row] - points[other]) / (points[col] - points[other])
                        )
                table[row, col] = value
    return table


def basis(where):
    points = gll_points()
    values = []
    slopes = []
    for node in range(5):
        value = jnp.ones_like(where)
        slope = jnp.zeros_like(where)
        for other in range(5):
            if other != node:
                scale = 1.0 / (points[node] - points[other])
                factor = (where - points[other]) * scale
                slope = slope * factor + value * scale
                value = value * factor
        values.append(value)
        slopes.append(slope)
    return (jnp.stack(values), jnp.stack(slopes))


def sources(resid, coord, angle, live_count):
    slots = resid.shape[-1]
    live = jnp.arange(slots, dtype=jnp.int32)[None, :] < live_count[:, None]
    value = jnp.where(live, resid, 0.0).reshape(-1)
    first = coord[:, 0, :].reshape(-1)
    second = coord[:, 1, :].reshape(-1)
    third = coord[:, 2, :].reshape(-1)
    azimuth = angle[:, 0, :].reshape(-1)
    dip = angle[:, 1, :].reshape(-1)
    tang_x = jnp.cos(azimuth) * jnp.cos(dip)
    tang_y = jnp.sin(azimuth) * jnp.cos(dip)
    tang_z = jnp.sin(dip)
    val_x, der_x = basis(first)
    val_y, der_y = basis(second)
    val_z, der_z = basis(third)
    shape = (
        tang_x * der_x[:, None, None, :] * val_y[None, :, None, :] * val_z[None, None, :, :]
        + tang_y * val_x[:, None, None, :] * der_y[None, :, None, :] * val_z[None, None, :, :]
        + tang_z * val_x[:, None, None, :] * val_y[None, :, None, :] * der_z[None, None, :, :]
    )
    direction = jnp.stack([tang_x, tang_y, tang_z]) * value[None, :]
    return (direction[:, None, None, None, :] * shape[None]).reshape(375, -1)


def along(field, table, dim):
    if dim == 0:
        return jnp.einsum("pa,...aqsz->...pqsz", table, field, precision=lax.Precision.HIGHEST)
    if dim == 1:
        return jnp.einsum("qb,...pbsz->...pqsz", table, field, precision=lax.Precision.HIGHEST)
    return jnp.einsum("sc,...pqcz->...pqsz", table, field, precision=lax.Precision.HIGHEST)


def back(field, table, dim):
    if dim == 0:
        return jnp.einsum("pa,...pqsz->...aqsz", table, field, precision=lax.Precision.HIGHEST)
    if dim == 1:
        return jnp.einsum("qb,...pqsz->...pbsz", table, field, precision=lax.Precision.HIGHEST)
    return jnp.einsum("sc,...pqsz->...pqcz", table, field, precision=lax.Precision.HIGHEST)


def stiffness(field, moduli):
    table = jnp.asarray(derivative_table(), jnp.float32)
    weight = jnp.asarray(gll_weights(), jnp.float32)
    wgrid = (weight[:, None, None] * weight[None, :, None] * weight[None, None, :])[:, :, :, None]
    grads = [along(field, table, dim) for dim in range(3)]
    lame = moduli[..., 0, :][..., None, None, None, :]
    shear = moduli[..., 1, :][..., None, None, None, :]
    diverge = (
        grads[0][..., 0, :, :, :, :] + grads[1][..., 1, :, :, :, :] + grads[2][..., 2, :, :, :, :]
    )
    result = jnp.zeros_like(field)
    for col in range(3):
        parts = []
        for row in range(3):
            stress = shear * (grads[col][..., row, :, :, :, :] + grads[row][..., col, :, :, :, :])
            if row == col:
                stress = stress + lame * diverge
            parts.append(stress * wgrid)
        result = result + back(jnp.stack(parts, axis=-5), table, col)
    return result


def assemble_dim(field, e_dim, n_dim, fetch):
    count = field.shape[e_dim]
    low = lax.slice_in_dim(field, 0, 1, axis=n_dim)
    high = lax.slice_in_dim(field, 4, 5, axis=n_dim)
    middle = lax.slice_in_dim(field, 1, 4, axis=n_dim)
    first = lax.slice_in_dim(low, 0, 1, axis=e_dim)
    last = lax.slice_in_dim(high, count - 1, count, axis=e_dim)
    below, above = fetch(first, last)
    low_next = jnp.concatenate([lax.slice_in_dim(low, 1, count, axis=e_dim), above], axis=e_dim)
    high_prev = jnp.concatenate(
        [below, lax.slice_in_dim(high, 0, count - 1, axis=e_dim)], axis=e_dim
    )
    return jnp.concatenate([low + high_prev, middle, high + low_next], axis=n_dim)


def fetch_none(first, last):
    return (jnp.zeros_like(last), jnp.zeros_like(first))


def fetch_first(first, last):
    padded = with_halo(jnp.concatenate([first, last], axis=0), (("gx", 0),), 1)
    return (padded[0:1], padded[3:4])


def fetch_second(first, last):
    padded = with_halo(jnp.concatenate([first, last], axis=1), (("gy", 1),), 1)
    return (padded[:, 0:1], padded[:, 3:4])


def body(wavefield, moduli, residuals, coords, angles, element_ids, counts):
    cells_x = wavefield.shape[0]
    cells_y = wavefield.shape[1]
    depth = wavefield.shape[4]
    groups_x = lax.axis_size("gx")
    groups_y = lax.axis_size("gy")
    owners = groups_x * groups_y
    slots = residuals.shape[2]
    blocks = owners // 16
    elements = cells_x * cells_y * depth
    field = wavefield.reshape(cells_x, cells_y, 3, 5, 5, 5, depth)
    internal = stiffness(field, moduli)
    floats = (
        lax.all_to_all(residuals, ("gx", "gy"), split_axis=1, concat_axis=0, tiled=True),
        lax.all_to_all(coords, ("gx", "gy"), split_axis=1, concat_axis=0, tiled=True),
        lax.all_to_all(angles, ("gx", "gy"), split_axis=1, concat_axis=0, tiled=True),
    )
    index = (
        lax.all_to_all(element_ids, ("gx", "gy"), split_axis=1, concat_axis=0, tiled=True),
        lax.all_to_all(counts, ("gx", "gy"), split_axis=1, concat_axis=0, tiled=True),
    )
    got_resid = floats[0].reshape(blocks, 16, slots)
    got_coord = floats[1].reshape(blocks, 16, 3, slots)
    got_angle = floats[2].reshape(blocks, 16, 2, slots)
    got_ids = index[0].reshape(blocks, 16, slots)
    got_count = index[1].reshape(blocks, 16)
    numbers = jnp.arange(elements, dtype=jnp.int32)

    def add_block(step, total):
        contrib = sources(got_resid[step], got_coord[step], got_angle[step], got_count[step])
        onehot = (got_ids[step].reshape(-1)[:, None] == numbers[None, :]).astype(jnp.float32)
        onehot = onehot.reshape(-1, cells_x, cells_y, depth)
        return total + jnp.einsum("ks,sxyz->xykz", contrib, onehot, precision=lax.Precision.HIGHEST)

    start = jnp.zeros((cells_x, cells_y, 375, depth), jnp.float32)
    total = lax.fori_loop(0, blocks, add_block, start)
    injected = total.reshape(cells_x, cells_y, 3, 5, 5, 5, depth)
    force = injected - internal
    force = assemble_dim(force, 0, 3, fetch_first)
    force = assemble_dim(force, 1, 4, fetch_second)
    force = assemble_dim(force, 6, 5, fetch_none)
    return force.reshape(cells_x, cells_y, 3, 125, depth)


def solution(mesh):
    in_specs = (
        P("gx", "gy", None, None, None),
        P("gx", "gy", None, None),
        P(("gx", "gy"), None, None),
        P(("gx", "gy"), None, None, None),
        P(("gx", "gy"), None, None, None),
        P(("gx", "gy"), None, None),
        P(("gx", "gy"), None),
    )
    out_specs = P("gx", "gy", None, None, None)
    return jax.shard_map(body, mesh=mesh, in_specs=in_specs, out_specs=out_specs, check_vma=False)
```

profile of v0, /device:TPU:9, one launch (start us, length us, event | category | flops | bytes accessed | tf_op | source)
XLA Modules:
  0.0 154.2 jit_solution(17965460843285024868)
XLA Ops:
  1.5 6.3 %all-to-all-start.2 = ((s32[1,32,1]{2,0,1:T(1,128)}), s32[1,32,1]{2,0,1:T(1,128)S(1)}, u32[]{:S(2)}, u32[]{:S(2)}) async-start(s32[1,32,1]{2,0,1:T(1,128)} %copy.67), calls=%async_computation.2 | async-start | bytes 32768 | tf_op jit(solution)/shard_map/all_to_all | solution.py:179
  7.8 3.1 %fusion.33 = f32[5,2,2,3,5,5,256]{6,0,5,4,3,2,1:T(8,128)S(1)} fusion(f32[5,5,1,1,1,1,1]{1,0,6,5,4,3,2:T(8,128)} %constant.255, f32[2,2,3,5,5,5,256]{6,1,5,4,3,2,0:T(2,128)S(1)} %bitcast.111), kind=kOutput, calls=%fused_computation.120 | convolution fusion | flops 23040000 | bytes 3072100 | tf_op jit(solution)/shard_map/sc,...pqcz->...pqsz/dot_general | solution.py:98
  10.9 2.2 %fusion.35 = f32[5,2,2,3,5,5,256]{6,0,5,4,3,2,1:T(8,128)S(1)} fusion(f32[5,5,1,1,1,1,1]{1,0,6,5,4,3,2:T(8,128)S(1)} %copy-done.9, f32[2,2,3,5,5,5,256]{6,1,5,4,3,2,0:T(2,128)S(1)} %bitcast.110), kind=kOutput, calls=%fused_computation.123 | convolution fusion | flops 23040000 | bytes 3072100 | tf_op jit(solution)/shard_map/qb,...pbsz->...pqsz/dot_general | solution.py:97
  13.2 2.2 %fusion.41 = f32[2,2,3,5,5,5,256]{6,3,5,4,2,1,0:T(8,128)S(1)} fusion(f32[5,5,1,1,1,1,1]{1,0,6,5,4,3,2:T(8,128)S(1)} %copy-done.9, f32[2,2,3,5,5,5,256]{6,1,5,4,3,2,0:T(2,128)S(1)} %bitcast.109), kind=kOutput, calls=%fused_computation.127 | convolution fusion | flops 23040000 | bytes 3072100 | tf_op jit(solution)/shard_map/pa,...aqsz->...pqsz/dot_general | solution.py:95
  18.5 1.7 %add_multiply_fusion.2 = (f32[2,2,1,5,5,5,256]{6,3,5,4,2,1,0:T(8,128)}, f32[2,2,1,5,5,5,256]{6,3,5,4,2,1,0:T(8,128)}, f32[2,2,1,5,5,5,256]{6,3,5,4,2,1,0:T(8,128...) fusion(f32[2,2,3,5,5,5,256]{6,3,5,4,2,1,0:T(8,128)S(1)} %fusion.41, ...), kind=kLoop, calls=%fused_computation.139 | loop fusion | flops 2048000 | bytes 7176692 | tf_op jit(solution)/shard_map/mul | solution.py:126
  20.2 5.9 %all-to-all-start.3 = ((f32[1,32,128]{2,0,1:T(1,128)}), f32[1,32,128]{2,0,1:T(1,128)}, u32[]{:S(2)}, u32[]{:S(2)}) async-start(f32[1,32,128]{2,0,1:T(1,128)} %bitcast.5), calls=%async_computation.3 | async-start | bytes 32768 | tf_op jit(solution)/shard_map/all_to_all | solution.py:173
  26.1 3.1 %add_multiply_fusion.1 = (f32[2,2,1,5,5,5,256]{6,3,5,4,2,1,0:T(8,128)}, f32[2,2,1,5,5,5,256]{6,3,5,4,2,1,0:T(8,128)}) fusion(f32[2,2,1,5,5,5,256]{6,3,5,4,2,1,0:T(8,128)} %get-tuple-element.358, f32[2,2,3,5,5,5,256]{6,3,5,4,2,1,0:T(8,128)} %bitcast.115, f32[5,5,5]{0,2,1:T(8,128)S(1)} %broadcast_multiply_fusion.8, f32[2,2,256]{2,1,0:T(2,128)S(1)} %get-tuple-element.425, ...), kind=kLoop, calls=%fused_computation.138 | loop fusion | flops 1024000 | bytes 2564596 | tf_op jit(solution)/shard_map/mul | solution.py:126
  29.1 2.5 %all-to-all-done.3 = f32[1,32,128]{2,0,1:T(1,128)} async-done(((f32[1,32,128]{2,0,1:T(1,128)}), f32[1,32,128]{2,0,1:T(1,128)}, u32[]{:S(2)}, u32[]{:S(2)}) %all-to-all-start.3) | async-done | bytes 16416 | tf_op jit(solution)/shard_map/all_to_all | solution.py:173
  31.7 4.5 %all-to-all-start = ((s32[1,32,128]{2,0,1:T(1,128)}), s32[1,32,128]{2,0,1:T(1,128)}, u32[]{:S(2)}, u32[]{:S(2)}) async-start(s32[1,32,128]{2,0,1:T(1,128)} %bitcast), calls=%async_computation | async-start | bytes 32768 | tf_op jit(solution)/shard_map/all_to_all | solution.py:178
  36.2 4.6 %pad_maximum_fusion = (f32[2,2,3,5,5,5,256]{6,3,5,4,2,1,0:T(8,128)}, f32[2,2,3,5,5,5,256]{6,3,5,4,2,1,0:T(8,128)}) fusion(f32[2,2,1,5,5,5,256]{6,3,5,4,2,1,0:T(8,128)} %get-tuple-element.403, f32[2,2,1,5,5,5,256]{6,3,5,4,2,1,0:T(8,128)} %get-tuple-element.418, f32[2,2,1,5,5,5,256]{6,3,5,4,2,1,0:T(8,128)S(1)} %get-tuple-element.401, ...), kind=kLoop, calls=%fused_computation.107 | loop fusion | flops 1536000 | bytes 5632000 | tf_op jit(solution)/shard_map/stack | solution.py:127
  41.8 5.6 %all-to-all-start.4 = ((f32[1,32,3,128]{3,2,0,1:T(4,128)}), f32[1,32,3,128]{3,2,0,1:T(4,128)S(1)}, u32[]{:S(2)}, u32[]{:S(2)}) async-start(f32[1,32,3,128]{3,2,0,1:T(4,128)} %copy.69), calls=%async_computation.4 | async-start | bytes 131072 | tf_op jit(solution)/shard_map/all_to_all | solution.py:174
  47.4 5.9 %fusion.31 = f32[2,2,3,5,5,256,5]{5,6,4,3,2,1,0:T(8,128)} fusion(f32[5,5,1,1,1,1,1]{1,0,6,5,4,3,2:T(8,128)S(1)} %copy-done.9, f32[2,2,3,5,5,5,256]{6,3,5,4,2,1,0:T(8,128)} %get-tuple-element.420), kind=kOutput, calls=%fused_computation.117 | convolution fusion | flops 23040000 | bytes 3072100 | tf_op jit(solution)/shard_map/qb,...pqsz->...pbsz/dot_general | solution.py:105
  53.3 5.8 %all-to-all-start.1 = ((f32[1,32,2,128]{3,2,0,1:T(2,128)}), f32[1,32,2,128]{3,2,0,1:T(2,128)S(1)}, u32[]{:S(2)}, u32[]{:S(2)}) async-start(f32[1,32,2,128]{3,2,0,1:T(2,128)} %bitcast.2), calls=%async_computation.1 | async-start | bytes 65536 | tf_op jit(solution)/shard_map/all_to_all | solution.py:175
  59.1 5.9 %fusion.29 = f32[2,2,3,5,5,256,5]{5,6,4,3,2,1,0:T(8,128)} fusion(f32[5,5,1,1,1,1,1]{1,0,6,5,4,3,2:T(8,128)S(1)} %copy-done.9, f32[2,2,3,5,5,5,256]{6,3,5,4,2,1,0:T(8,128)} %get-tuple-element.421), kind=kOutput, calls=%fused_computation.115 | convolution fusion | flops 23040000 | bytes 3072100 | tf_op jit(solution)/shard_map/sc,...pqsz->...pqcz/dot_general | solution.py:106
  65.8 52.7 %while.17 = (s32[]{:T(128)}, f32[2,2,375,256]{3,2,1,0:T(8,128)}, s32[2,16,128]{2,1,0:T(8,128)}, f32[2,16,2,128]{3,2,1,0:T(2,128)S(1)}, s32[2,16]{1,0:T(2,128)S(1...) while((s32[]{:T(128)}, f32[2,2,375,256]{3,2,1,0:T(8,128)}, ...), condition=%wide.region_1.2_spmd.clone, body=%wide.region_0.1_spmd.clone.sunk | while | flops 9442392064 | bytes 20555300 | solution.py:195
  71.9 1.5 multiply_multiply_fusion.38
  75.5 2.9 %broadcast_multiply_fusion.15 = f32[3,5,5,5,2048]{4,3,2,1,0:T(8,128)} fusion(f32[5,5,5,2048]{3,2,1,0:T(8,128)S(1)} %multiply_add_fusion.22, f32[3,2048]{1,0:T(4,128)S(1)} %maximum_multiply_fusion.2), kind=kLoop, calls=%fused_computation.6.clone.1 | loop fusion | flops 768000 | bytes 4120576 | tf_op jit(solution)/shard_map/while/body/eval_jaxpr/mul | solution.py:90
  78.4 5.1 %reshape.2477 = f32[375,2048,1,1]{1,0,2,3:T(8,128)} reshape(f32[3,5,5,5,2048]{4,3,2,1,0:T(8,128)} %broadcast_multiply_fusion.15) | data formatting | bytes 6144000 | tf_op jit(solution)/shard_map/while/body/eval_jaxpr/mul | solution.py:90
  83.4 8.3 %bitcast_add_fusion.4 = f32[2,2,375,256]{3,2,1,0:T(8,128)} fusion(f32[2,2,375,256]{3,2,1,0:T(8,128)} %get-tuple-element.563, f32[375,2048,1,1]{1,0,2,3:T(8,128)} %reshape.2477, s32[2,2,256]{2,1,0:T(2,128)S(1)} %copy-done.10, s32[2048]{0:T(1024)S(1)} %copy-done.8, pred[]{:T(512)S(6)} %compare.5), kind=kOutput, calls=%fused_computation.8.clone.1 | convolution fusion | flops 9440049152 | bytes 6156289 | tf_op jit(solution)/shard_map/while/body/eval_jaxpr/ks,sxyz->xykz/dot_general | solution.py:192
  101.5 2.9 %broadcast_multiply_fusion.15 = f32[3,5,5,5,2048]{4,3,2,1,0:T(8,128)} fusion(f32[5,5,5,2048]{3,2,1,0:T(8,128)S(1)} %multiply_add_fusion.22, f32[3,2048]{1,0:T(4,128)S(1)} %maximum_multiply_fusion.2), kind=kLoop, calls=%fused_computation.6.clone.1 | loop fusion | flops 768000 | bytes 4120576 | tf_op jit(solution)/shard_map/while/body/eval_jaxpr/mul | solution.py:90
  104.4 5.1 %reshape.2477 = f32[375,2048,1,1]{1,0,2,3:T(8,128)} reshape(f32[3,5,5,5,2048]{4,3,2,1,0:T(8,128)} %broadcast_multiply_fusion.15) | data formatting | bytes 6144000 | tf_op jit(solution)/shard_map/while/body/eval_jaxpr/mul | solution.py:90
  109.5 8.8 %bitcast_add_fusion.4 = f32[2,2,375,256]{3,2,1,0:T(8,128)} fusion(f32[2,2,375,256]{3,2,1,0:T(8,128)} %get-tuple-element.563, f32[375,2048,1,1]{1,0,2,3:T(8,128)} %reshape.2477, s32[2,2,256]{2,1,0:T(2,128)S(1)} %copy-done.10, s32[2048]{0:T(1024)S(1)} %copy-done.8, pred[]{:T(512)S(6)} %compare.5), kind=kOutput, calls=%fused_computation.8.clone.1 | convolution fusion | flops 9440049152 | bytes 6156289 | tf_op jit(solution)/shard_map/while/body/eval_jaxpr/ks,sxyz->xykz/dot_general | solution.py:192
  118.5 2.3 %copy.73 = f32[2,2,375,256]{3,1,2,0:T(2,128)S(1)} copy(f32[2,2,375,256]{3,2,1,0:T(8,128)} %get-tuple-element.295) | data formatting | bytes 3072000 | tf_op jit(solution)/shard_map/while | solution.py:195
  120.9 5.7 %fusion.28 = f32[2,2,3,5,5,5,256]{6,3,5,4,2,1,0:T(8,128)S(1)} fusion(f32[2,2,3,5,5,5,256]{6,1,5,4,3,2,0:T(2,128)S(1)} %bitcast.116, f32[2,2,3,5,5,256,5]{5,6,4,3,2,1,0:T(8,128)} %fusion.29, f32[2,2,3,5,5,256,5]{5,6,4,3,2,1,0:T(8,128)S(1)} %copy-done.3, f32[5,5,1,1,1,1,1]{1,0,6,5,4,3,2:T(8,128)S(1)} %copy-done.9, ...), kind=kOutput, calls=%fused_computation.113 | convolution fusion | flops 24960000 | bytes 7680100 | tf_op jit(solution)/shard_map/pa,...pqsz->...aqsz/dot_general | solution.py:103
  127.1 3.4 %collective-permute-start = (f32[1,2,3,1,5,5,256]{6,3,5,4,2,1,0:T(1,128)S(1)}, f32[1,2,3,1,5,5,256]{6,3,5,4,2,1,0:T(1,128)S(1)}, u32[]{:S(2)}, u32[]{:S(2)}) collective-permute-start(f32[1,2,3,1,5,5,256]{6,3,5,4,2,1,0:T(1,128)S(1)} %get-tuple-element.412), channel_id=1, source_target_pairs={{0,8},{8,16},{16,24},{1,9},{9,17},{17,25},{2,10},{10,18},{18,26},{... | collective-permute-start | bytes 460808 | tf_op jit(solution)/shard_map/ppermute | solution.py:15
  130.5 1.9 %collective-permute-start.1 = (f32[1,2,3,1,5,5,256]{6,3,5,4,2,1,0:T(1,128)S(1)}, f32[1,2,3,1,5,5,256]{6,3,5,4,2,1,0:T(1,128)S(1)}, u32[]{:S(2)}, u32[]{:S(2)}) collective-permute-start(f32[1,2,3,1,5,5,256]{6,3,5,4,2,1,0:T(1,128)S(1)} %get-tuple-element.413), channel_id=1, source_target_pairs={{8,0},{16,8},{24,16},{9,1},{17,9},{25,17},{10,2},{18,10},{26,18},{... | collective-permute-start | bytes 460808 | tf_op jit(solution)/shard_map/ppermute | solution.py:18
  132.7 4.3 %collective-permute-done.1 = f32[1,2,3,1,5,5,256]{6,3,5,4,2,1,0:T(1,128)S(1)} collective-permute-done((f32[1,2,3,1,5,5,256]{6,3,5,4,2,1,0:T(1,128)S(1)}, f32[1,2,3,1,5,5,256]{6,3,5,4,2,1,0:T(1,128)S(1)}, u32[]{:S(2)}, u32[]{:S(2)}) %collective-permute-start.1) | collective-permute-done | bytes 153632 | tf_op jit(solution)/shard_map/ppermute | solution.py:18
  138.0 3.1 %collective-permute-start.2 = (f32[2,1,3,5,1,5,256]{6,3,5,4,2,1,0:T(8,128)S(1)}, f32[2,1,3,5,1,5,256]{6,3,5,4,2,1,0:T(8,128)S(1)}, u32[]{:S(2)}, u32[]{:S(2)}) collective-permute-start(f32[2,1,3,5,1,5,256]{6,3,5,4,2,1,0:T(8,128)S(1)} %get-tuple-element.416), channel_id=1, source_target_pairs={{0,1},{1,2},{2,3},{3,4},{4,5},{5,6},{6,7},{8,9},{9,10},{10,11},{11... | collective-permute-start | bytes 460808 | tf_op jit(solution)/shard_map/ppermute | solution.py:15
  141.1 3.1 %collective-permute-start.3 = (f32[2,1,3,5,1,5,256]{6,3,5,4,2,1,0:T(8,128)S(1)}, f32[2,1,3,5,1,5,256]{6,3,5,4,2,1,0:T(8,128)S(1)}, u32[]{:S(2)}, u32[]{:S(2)}) collective-permute-start(f32[2,1,3,5,1,5,256]{6,3,5,4,2,1,0:T(8,128)S(1)} %get-tuple-element.417), channel_id=1, source_target_pairs={{1,0},{2,1},{3,2},{4,3},{5,4},{6,5},{7,6},{9,8},{10,9},{11,10},{12... | collective-permute-start | bytes 460808 | tf_op jit(solution)/shard_map/ppermute | solution.py:18
  145.1 4.4 %collective-permute-done.2 = f32[2,1,3,5,1,5,256]{6,3,5,4,2,1,0:T(8,128)S(1)} collective-permute-done((f32[2,1,3,5,1,5,256]{6,3,5,4,2,1,0:T(8,128)S(1)}, f32[2,1,3,5,1,5,256]{6,3,5,4,2,1,0:T(8,128)S(1)}, u32[]{:S(2)}, u32[]{:S(2)}) %collective-permute-start.2) | collective-permute-done | bytes 153632 | tf_op jit(solution)/shard_map/ppermute | solution.py:15
  149.4 1.6 %collective-permute-done.3 = f32[2,1,3,5,1,5,256]{6,3,5,4,2,1,0:T(8,128)S(1)} collective-permute-done((f32[2,1,3,5,1,5,256]{6,3,5,4,2,1,0:T(8,128)S(1)}, f32[2,1,3,5,1,5,256]{6,3,5,4,2,1,0:T(8,128)S(1)}, u32[]{:S(2)}, u32[]{:S(2)}) %collective-permute-start.3) | collective-permute-done | bytes 153632 | tf_op jit(solution)/shard_map/ppermute | solution.py:18
  152.3 1.9 %copy.87 = f32[2,2,3,5,5,5,256]{6,1,5,4,3,2,0:T(2,128)} copy(f32[2,2,3,5,5,5,256]{6,3,5,4,2,1,0:T(8,128)S(1)} %pad_maximum_fusion.4) | data formatting | bytes 3072000 | tf_op jit(solution)/shard_map/concatenate | solution.py:143
  (120 shorter events, 28.0 us)
Async XLA Ops:
  0.0 7.8 %copy-start = (f32[2,2,3,125,256]{4,1,3,2,0:T(2,128)S(1)}, f32[2,2,3,125,256]{4,1,3,2,0:T(2,128)}, u32[]{:S(2)}) copy-start(f32[2,2,3,125,256]{4,1,3,2,0:T(2,128)} %param.11) | copy-start | bytes 4608004
  1.5 18.7 %all-to-all-start.2 = ((s32[1,32,1]{2,0,1:T(1,128)}), s32[1,32,1]{2,0,1:T(1,128)S(1)}, u32[]{:S(2)}, u32[]{:S(2)}) async-start(s32[1,32,1]{2,0,1:T(1,128)} %copy.67), calls=%async_computation.2 | async-start | bytes 32768 | tf_op jit(solution)/shard_map/all_to_all | solution.py:179
  7.8 3.1 %copy-start.9 = (f32[5,5,1,1,1,1,1]{1,0,6,5,4,3,2:T(8,128)S(1)}, f32[5,5,1,1,1,1,1]{1,0,6,5,4,3,2:T(8,128)}, u32[]{:S(2)}) copy-start(f32[5,5,1,1,1,1,1]{1,0,6,5,4,3,2:T(8,128)} %constant.255) | copy-start | bytes 304
  13.1 2.3 %copy-start.13 = (f32[5]{0:T(128)S(1)}, f32[5]{0:T(128)}, u32[]{:S(2)}) copy-start(f32[5]{0:T(128)} %constant.241.clone) | copy-start | bytes 64
  13.2 2.3 %copy-start.12 = (f32[2,2,2,256]{3,2,1,0:T(2,128)S(1)}, f32[2,2,2,256]{3,2,1,0:T(2,128)}, u32[]{:S(2)}) copy-start(f32[2,2,2,256]{3,2,1,0:T(2,128)} %param.12) | copy-start | bytes 24580
  17.0 1.6 %copy-start.2 = (f32[5,2,2,3,5,5,256]{6,4,5,0,3,2,1:T(8,128)}, f32[5,2,2,3,5,5,256]{6,4,5,0,3,2,1:T(8,128)S(1)}, u32[]{:S(2)}) copy-start(f32[5,2,2,3,5,5,256]{6,4,5,0,3,2,1:T(8,128)S(1)} %copy.125) | copy-start | bytes 4608004
  20.2 11.5 %all-to-all-start.3 = ((f32[1,32,128]{2,0,1:T(1,128)}), f32[1,32,128]{2,0,1:T(1,128)}, u32[]{:S(2)}, u32[]{:S(2)}) async-start(f32[1,32,128]{2,0,1:T(1,128)} %bitcast.5), calls=%async_computation.3 | async-start | bytes 32768 | tf_op jit(solution)/shard_map/all_to_all | solution.py:173
  31.7 10.2 %all-to-all-start = ((s32[1,32,128]{2,0,1:T(1,128)}), s32[1,32,128]{2,0,1:T(1,128)}, u32[]{:S(2)}, u32[]{:S(2)}) async-start(s32[1,32,128]{2,0,1:T(1,128)} %bitcast), calls=%async_computation | async-start | bytes 32768 | tf_op jit(solution)/shard_map/all_to_all | solution.py:178
  36.2 4.6 %copy-start.11 = (f32[1,32,3,128]{3,1,2,0:T(8,128)S(1)}, f32[1,32,3,128]{3,1,2,0:T(8,128)}, u32[]{:S(2)}) copy-start(f32[1,32,3,128]{3,1,2,0:T(8,128)} %param.14) | copy-start | bytes 147460
  41.8 11.5 %all-to-all-start.4 = ((f32[1,32,3,128]{3,2,0,1:T(4,128)}), f32[1,32,3,128]{3,2,0,1:T(4,128)S(1)}, u32[]{:S(2)}, u32[]{:S(2)}) async-start(f32[1,32,3,128]{3,2,0,1:T(4,128)} %copy.69), calls=%async_computation.4 | async-start | bytes 131072 | tf_op jit(solution)/shard_map/all_to_all | solution.py:174
  53.3 12.5 %all-to-all-start.1 = ((f32[1,32,2,128]{3,2,0,1:T(2,128)}), f32[1,32,2,128]{3,2,0,1:T(2,128)S(1)}, u32[]{:S(2)}, u32[]{:S(2)}) async-start(f32[1,32,2,128]{3,2,0,1:T(2,128)} %bitcast.2), calls=%async_computation.1 | async-start | bytes 65536 | tf_op jit(solution)/shard_map/all_to_all | solution.py:175
  65.8 2.7 %copy-start.14 = (s32[2,16]{1,0:T(2,128)}, s32[2,16]{1,0:T(2,128)S(1)}, u32[]{:S(2)}) copy-start(s32[2,16]{1,0:T(2,128)S(1)} %get-tuple-element.575) | copy-start | bytes 388 | tf_op jit(solution)/shard_map/while
  65.8 4.3 %copy-start.4 = (f32[2,16,3,128]{3,1,2,0:T(8,128)}, f32[2,16,3,128]{3,1,2,0:T(8,128)S(1)}, u32[]{:S(2)}) copy-start(f32[2,16,3,128]{3,1,2,0:T(8,128)S(1)} %get-tuple-element.577) | copy-start | bytes 147460 | tf_op jit(solution)/shard_map/while
  65.8 4.3 %copy-start.6 = (f32[2,16,2,128]{3,2,1,0:T(2,128)}, f32[2,16,2,128]{3,2,1,0:T(2,128)S(1)}, u32[]{:S(2)}) copy-start(f32[2,16,2,128]{3,2,1,0:T(2,128)S(1)} %get-tuple-element.574) | copy-start | bytes 98308 | tf_op jit(solution)/shard_map/while
  78.4 5.1 %copy-start.8 = (s32[2048]{0:T(1024)S(1)}, s32[2048]{0:T(1024)}, u32[]{:S(2)}) copy-start(s32[2048]{0:T(1024)} %dynamic-slice_bitcast_fusion.5) | copy-start | bytes 24580 | tf_op jit(solution)/shard_map/while
  78.4 5.1 %copy-start.10 = (s32[2,2,256]{2,1,0:T(2,128)S(1)}, s32[2,2,256]{2,1,0:T(2,128)}, u32[]{:S(2)}) copy-start(s32[2,2,256]{2,1,0:T(2,128)} %multiply_add_fusion.23) | copy-start | bytes 12292 | tf_op jit(solution)/shard_map/while
  83.4 8.4 %copy-start.5 = (f32[2,16,3,128]{3,1,2,0:T(8,128)S(1)}, f32[2,16,3,128]{3,1,2,0:T(8,128)}, u32[]{:S(2)}) copy-start(f32[2,16,3,128]{3,1,2,0:T(8,128)} %copy-done.4) | copy-start | bytes 147460 | tf_op jit(solution)/shard_map/while
  83.4 8.4 %copy-start.7 = (f32[2,16,2,128]{3,2,1,0:T(2,128)S(1)}, f32[2,16,2,128]{3,2,1,0:T(2,128)}, u32[]{:S(2)}) copy-start(f32[2,16,2,128]{3,2,1,0:T(2,128)} %copy-done.6) | copy-start | bytes 98308 | tf_op jit(solution)/shard_map/while
  83.4 8.4 %copy-start.15 = (s32[2,16]{1,0:T(2,128)S(1)}, s32[2,16]{1,0:T(2,128)}, u32[]{:S(2)}) copy-start(s32[2,16]{1,0:T(2,128)} %copy-done.14) | copy-start | bytes 388 | tf_op jit(solution)/shard_map/while
  91.8 2.7 %copy-start.14 = (s32[2,16]{1,0:T(2,128)}, s32[2,16]{1,0:T(2,128)S(1)}, u32[]{:S(2)}) copy-start(s32[2,16]{1,0:T(2,128)S(1)} %get-tuple-element.575) | copy-start | bytes 388 | tf_op jit(solution)/shard_map/while
  91.8 4.3 %copy-start.4 = (f32[2,16,3,128]{3,1,2,0:T(8,128)}, f32[2,16,3,128]{3,1,2,0:T(8,128)S(1)}, u32[]{:S(2)}) copy-start(f32[2,16,3,128]{3,1,2,0:T(8,128)S(1)} %get-tuple-element.577) | copy-start | bytes 147460 | tf_op jit(solution)/shard_map/while
  91.8 4.3 %copy-start.6 = (f32[2,16,2,128]{3,2,1,0:T(2,128)}, f32[2,16,2,128]{3,2,1,0:T(2,128)S(1)}, u32[]{:S(2)}) copy-start(f32[2,16,2,128]{3,2,1,0:T(2,128)S(1)} %get-tuple-element.574) | copy-start | bytes 98308 | tf_op jit(solution)/shard_map/while
  104.4 5.1 %copy-start.8 = (s32[2048]{0:T(1024)S(1)}, s32[2048]{0:T(1024)}, u32[]{:S(2)}) copy-start(s32[2048]{0:T(1024)} %dynamic-slice_bitcast_fusion.5) | copy-start | bytes 24580 | tf_op jit(solution)/shard_map/while
  104.4 5.1 %copy-start.10 = (s32[2,2,256]{2,1,0:T(2,128)S(1)}, s32[2,2,256]{2,1,0:T(2,128)}, u32[]{:S(2)}) copy-start(s32[2,2,256]{2,1,0:T(2,128)} %multiply_add_fusion.23) | copy-start | bytes 12292 | tf_op jit(solution)/shard_map/while
  109.4 8.8 %copy-start.5 = (f32[2,16,3,128]{3,1,2,0:T(8,128)S(1)}, f32[2,16,3,128]{3,1,2,0:T(8,128)}, u32[]{:S(2)}) copy-start(f32[2,16,3,128]{3,1,2,0:T(8,128)} %copy-done.4) | copy-start | bytes 147460 | tf_op jit(solution)/shard_map/while
  109.4 8.8 %copy-start.7 = (f32[2,16,2,128]{3,2,1,0:T(2,128)S(1)}, f32[2,16,2,128]{3,2,1,0:T(2,128)}, u32[]{:S(2)}) copy-start(f32[2,16,2,128]{3,2,1,0:T(2,128)} %copy-done.6) | copy-start | bytes 98308 | tf_op jit(solution)/shard_map/while
  109.5 8.8 %copy-start.15 = (s32[2,16]{1,0:T(2,128)S(1)}, s32[2,16]{1,0:T(2,128)}, u32[]{:S(2)}) copy-start(s32[2,16]{1,0:T(2,128)} %copy-done.14) | copy-start | bytes 388 | tf_op jit(solution)/shard_map/while
  118.5 2.4 %copy-start.3 = (f32[2,2,3,5,5,256,5]{5,6,4,3,2,1,0:T(8,128)S(1)}, f32[2,2,3,5,5,256,5]{5,6,4,3,2,1,0:T(8,128)}, u32[]{:S(2)}) copy-start(f32[2,2,3,5,5,256,5]{5,6,4,3,2,1,0:T(8,128)} %fusion.31) | copy-start | bytes 4608004
  127.1 5.6 %collective-permute-start = (f32[1,2,3,1,5,5,256]{6,3,5,4,2,1,0:T(1,128)S(1)}, f32[1,2,3,1,5,5,256]{6,3,5,4,2,1,0:T(1,128)S(1)}, u32[]{:S(2)}, u32[]{:S(2)}) collective-permute-start(f32[1,2,3,1,5,5,256]{6,3,5,4,2,1,0:T(1,128)S(1)} %get-tuple-element.412), channel_id=1, source_target_pairs={{0,8},{8,16},{16,24},{1,9},{9,17},{17,25},{2,10},{10,18},{18,26},{... | collective-permute-start | bytes 460808 | tf_op jit(solution)/shard_map/ppermute | solution.py:15
  130.5 6.5 %collective-permute-start.1 = (f32[1,2,3,1,5,5,256]{6,3,5,4,2,1,0:T(1,128)S(1)}, f32[1,2,3,1,5,5,256]{6,3,5,4,2,1,0:T(1,128)S(1)}, u32[]{:S(2)}, u32[]{:S(2)}) collective-permute-start(f32[1,2,3,1,5,5,256]{6,3,5,4,2,1,0:T(1,128)S(1)} %get-tuple-element.413), channel_id=1, source_target_pairs={{8,0},{16,8},{24,16},{9,1},{17,9},{25,17},{10,2},{18,10},{26,18},{... | collective-permute-start | bytes 460808 | tf_op jit(solution)/shard_map/ppermute | solution.py:18
  138.0 11.5 %collective-permute-start.2 = (f32[2,1,3,5,1,5,256]{6,3,5,4,2,1,0:T(8,128)S(1)}, f32[2,1,3,5,1,5,256]{6,3,5,4,2,1,0:T(8,128)S(1)}, u32[]{:S(2)}, u32[]{:S(2)}) collective-permute-start(f32[2,1,3,5,1,5,256]{6,3,5,4,2,1,0:T(8,128)S(1)} %get-tuple-element.416), channel_id=1, source_target_pairs={{0,1},{1,2},{2,3},{3,4},{4,5},{5,6},{6,7},{8,9},{9,10},{10,11},{11... | collective-permute-start | bytes 460808 | tf_op jit(solution)/shard_map/ppermute | solution.py:15
  141.1 10.0 %collective-permute-start.3 = (f32[2,1,3,5,1,5,256]{6,3,5,4,2,1,0:T(8,128)S(1)}, f32[2,1,3,5,1,5,256]{6,3,5,4,2,1,0:T(8,128)S(1)}, u32[]{:S(2)}, u32[]{:S(2)}) collective-permute-start(f32[2,1,3,5,1,5,256]{6,3,5,4,2,1,0:T(8,128)S(1)} %get-tuple-element.417), channel_id=1, source_target_pairs={{1,0},{2,1},{3,2},{4,3},{5,4},{6,5},{7,6},{9,8},{10,9},{11,10},{12... | collective-permute-start | bytes 460808 | tf_op jit(solution)/shard_map/ppermute | solution.py:18
  (1 other events, 1.5 us)
where the time goes:
time: 155 us; the launch traced here: 154 us
  matrix products  42.2 us (27%)
  starting transfers between devices  39.5 us (25%)
  other arithmetic  31.6 us (20%)
  local copies, waits for them, and re-layouts  26.9 us (17%)
  waiting for transfers between devices  13.2 us (9%)
    dot_general x2, matrix products, add_block(): jnp.einsum('ks,sxyz->xykz', contrib, onehot, precision=lax.Precision.HIGH...  17.1 us
    mul x2, local copies, waits for them, and re-layouts, sources(): return (direction[:, None, None, None, :] * shape[None]).reshape(375, -1)  10.1 us
    ppermute x2, starting transfers between devices, with_halo(): lax.ppermute(lax.slice_in_dim(block, block.shape[dim] - width, None, axis...  6.47 us
    all_to_all x1, starting transfers between devices, body(): lax.all_to_all(counts, ('gx', 'gy'), split_axis=1, concat_axis=0, tiled=T...  6.32 us
    dot_general x1, matrix products, back(): jnp.einsum('sc,...pqsz->...pqcz', table, field, precision=lax.Precision.H...  5.9 us
    all_to_all x1, starting transfers between devices, body(): lax.all_to_all(residuals, ('gx', 'gy'), split_axis=1, concat_axis=0, tile...  5.89 us
    dot_general x1, matrix products, back(): jnp.einsum('qb,...pqsz->...pbsz', table, field, precision=lax.Precision.H...  5.89 us
    ppermute x2, waiting for transfers between devices, with_halo(): lax.ppermute(lax.slice_in_dim(block, 0, width, axis=dim), axis, backward)  5.88 us
  transfers between devices with their start and end apart: 9, of which 5 were waited for; matrix products, arithmetic and copies ran while one was open for 21% of the time, Pallas kernels for 0%

commit v1 on v0

v1 whole, which is shorter than its diff:
```python
import functools
import math

import jax
import jax.numpy as jnp
import numpy as np
from jax import lax
from jax.experimental import pallas as pl
from jax.experimental.pallas import tpu as pltpu
from jax.sharding import PartitionSpec as P

MESH = pl.DeviceIdType.MESH
F32, BF16 = jnp.float32, jnp.bfloat16
PAD = 128
GROUP = 8


def gll_points():
    return np.array([-1.0, -math.sqrt(3.0 / 7.0), 0.0, math.sqrt(3.0 / 7.0), 1.0])


def gll_weights():
    return np.array([0.1, 49.0 / 90.0, 32.0 / 45.0, 49.0 / 90.0, 0.1])


def derivative_table():
    points = gll_points()
    table = np.zeros((5, 5))
    for row in range(5):
        for col in range(5):
            if row == col:
                table[row, col] = sum(
                    (1.0 / (points[col] - points[other]) for other in range(5) if other != col)
                )
            else:
                value = 1.0 / (points[col] - points[row])
                for other in range(5):
                    if other != col and other != row:
                        value = (
                            value * (points[row] - points[other]) / (points[col] - points[other])
                        )
                table[row, col] = value
    return table


def split_table(table):
    high = table.astype(BF16)
    return high, (table - high.astype(np.float64)).astype(BF16)


def tables():
    dm, eye = derivative_table(), np.eye(5)
    w1 = gll_weights()
    weight = (w1[:, None, None] * w1[None, :, None] * w1[None, None, :]).reshape(-1)
    dirs = [
        np.kron(np.kron(dm, eye), eye),
        np.kron(np.kron(eye, dm), eye),
        np.kron(np.kron(eye, eye), dm),
    ]
    grad = np.zeros((3 * PAD, PAD))
    back = np.zeros((PAD, 3 * PAD))
    for j in range(3):
        grad[j * PAD : j * PAD + 125, :125] = dirs[j]
        back[:125, j * PAD : j * PAD + 125] = -dirs[j].T * weight[None, :]
    gh, gl = split_table(grad)
    bh, bl = split_table(back)
    g1 = np.concatenate([gh, gh], 1)
    bs = np.concatenate([bh, bl], 0)
    spread = np.zeros((4 * PAD, 192))
    for p in range(5):
        for q in range(5):
            for r in range(5):
                n = (p * 5 + q) * 5 + r
                for base, col in ((0, p * 8 + q), (1, 40 + p * 8 + q), (2, 80 + r), (3, 88 + r)):
                    spread[base * PAD + n, col] = 1.0
                    spread[base * PAD + n, 96 + col] = 1.0
    points = gll_points()
    consts = np.zeros((8, 8, 128), np.float32)
    for q in range(5):
        others = [k for k in range(5) if k != q]
        for j, k in enumerate(others):
            consts[j, q] = points[k]
            consts[4 + j, q] = 1.0 / (points[q] - points[k])
    return (
        jnp.asarray(g1),
        jnp.asarray(gl),
        jnp.asarray(bs),
        jnp.asarray(spread.astype(BF16)),
        jnp.asarray(consts),
    )


def split(x):
    high = x.astype(BF16)
    return high, (x - high.astype(F32)).astype(BF16)


def dot(a, b):
    return jnp.dot(a, b, preferred_element_type=F32)


def dot_t(a, b):
    return lax.dot_general(a, b, (((1,), (1,)), ((), ())), preferred_element_type=F32)


def scatter_kernel(nx, ny, resid, coord, angle, ids, count, recv, packed, got, send_sem, recv_sem):
    n = nx * ny
    gx, gy = lax.axis_index("gx"), lax.axis_index("gy")
    me = gx * ny + gy
    barrier = pltpu.get_barrier_semaphore()

    def greet(k, c):
        to = lax.rem(me + k, n)
        pl.semaphore_signal(
            barrier, inc=1, device_id=(to // ny, lax.rem(to, ny)), device_id_type=MESH
        )
        return c

    lax.fori_loop(1, n, greet, 0)
    slots = resid.shape[2]
    rows = lax.broadcasted_iota(jnp.int32, (n, n), 0)
    cols = lax.broadcasted_iota(jnp.int32, (n, n), 1)
    spread = jnp.where(rows == cols, count[...].astype(F32), 0.0)
    live_count = jnp.sum(spread, axis=1, keepdims=True)
    slot = lax.broadcasted_iota(jnp.int32, (n, slots), 1).astype(F32)
    az, dip = angle[0, :, 0, :], angle[0, :, 1, :]
    cd = jnp.cos(dip)
    packed[:, 0, :] = jnp.where(slot < live_count, resid[0], 0.0)
    for d in range(3):
        packed[:, 1 + d, :] = coord[0, :, d, :]
    packed[:, 4, :] = jnp.cos(az) * cd
    packed[:, 5, :] = jnp.sin(az) * cd
    packed[:, 6, :] = jnp.sin(dip)
    packed[:, 7, :] = ids[0].astype(F32)
    pl.semaphore_wait(barrier, n - 1)

    def copy(k, to, at):
        return pltpu.make_async_remote_copy(
            src_ref=packed.at[to],
            dst_ref=got.at[at],
            send_sem=send_sem.at[k],
            recv_sem=recv_sem.at[k],
            device_id=(to // ny, lax.rem(to, ny)),
            device_id_type=MESH,
        )

    def send(k, c):
        copy(k, lax.rem(me + k, n), me).start()
        return c

    lax.fori_loop(1, n, send, 0)
    recv[me] = packed[me]

    def finish(k, c):
        frm = lax.rem(me - k + n, n)
        copy(k, lax.rem(me + k, n), frm).wait_recv()
        recv[frm] = got[frm]
        return c

    lax.fori_loop(1, n, finish, 0)

    def drain(k, c):
        copy(k, lax.rem(me + k, n), me).wait_send()
        return c

    lax.fori_loop(1, n, drain, 0)


def basis(row, const):
    x = jnp.broadcast_to(row, const[0].shape)
    value = slope = None
    for j in range(4):
        scale = const[4 + j]
        factor = (x - const[j]) * scale
        if value is None:
            value, slope = factor, scale
        else:
            slope = slope * factor + value * scale
            value = value * factor
    return value, slope


def force_kernel(
    cx, cy, u_ref, mod_ref, recv, g1, g2, bs, spread, consts, out, xs, ys, cs, acc, lhs, hot, pad
):
    n, slots = recv.shape[0], recv.shape[2]
    cells, depth = cx * cy, u_ref.shape[3]
    width = 2 * slots
    acc[...] = jnp.zeros_like(acc)
    pad[...] = jnp.zeros_like(pad)

    def block(b, carry):
        for pair in range(GROUP // 2):
            at = b * GROUP + 2 * pair
            tile = jnp.concatenate([recv[at], recv[at + 1]], axis=1)
            const = [
                jnp.concatenate([consts[j], consts[j]], axis=1) for j in range(8)
            ]
            v = tile[0:1]
            t = [tile[4 + i : 5 + i] for i in range(3)]
            lx, dx = basis(tile[1:2], const)
            ly, dy = basis(tile[2:3], const)
            lz, dz = basis(tile[3:4], const)
            dx, dy, dz = dx * t[0], dy * t[1], dz * t[2]
            first = [dx[p : p + 1] * ly + lx[p : p + 1] * dy for p in range(5)]
            second = [lx[p : p + 1] * ly for p in range(5)]
            high, low = split(jnp.concatenate(first + second + [lz, dz], axis=0))
            wide = dot(spread[...], jnp.concatenate([high, low], axis=0))
            shape = wide[:PAD] * wide[2 * PAD : 3 * PAD] + wide[PAD : 2 * PAD] * wide[3 * PAD :]
            cols = pl.ds(pair * width, width)
            for i in range(3):
                high, low = split(shape * (v * t[i]))
                lhs[i * PAD : (i + 1) * PAD, cols] = high
                lhs[(3 + i) * PAD : (4 + i) * PAD, cols] = low
            ident = tile[7:8].astype(jnp.int32)
            number = lax.broadcasted_iota(jnp.int32, (cells * depth, width), 0)
            hot[:, cols] = jnp.where(number == ident, 1.0, 0.0).astype(BF16)
        for cell in range(cells):
            got = dot_t(lhs[...], hot[cell * depth : (cell + 1) * depth, :])
            acc[cell] += got[: 3 * PAD] + got[3 * PAD :]
        return carry

    lax.fori_loop(0, n // GROUP, block, 0)

    node = lax.broadcasted_iota(jnp.int32, (PAD, depth), 0)
    lane = lax.broadcasted_iota(jnp.int32, (PAD, depth), 1)
    along = lax.rem(node, 5)
    take_up = (along == 4) & (lane < depth - 1)
    take_down = (along == 0) & (lane > 0)

    def stiff(cell, carry):
        g = []
        for c in range(3):
            pad[0:125, :] = u_ref[cell, c]
            high, low = split(pad[...])
            r = dot(g1[...], jnp.concatenate([high, low], axis=0)) + dot(g2[...], high)
            g.append([r[j * PAD : (j + 1) * PAD] for j in range(3)])
        lam, mu = mod_ref[cell, 0:1, :], mod_ref[cell, 1:2, :]
        press = lam * (g[0][0] + g[1][1] + g[2][2])
        for i in range(3):
            parts = []
            for j in range(3):
                s = mu * (g[i][j] + g[j][i])
                parts.append(s + press if i == j else s)
            high, low = split(jnp.concatenate(parts, axis=0))
            r = dot(bs[...], high)
            r = r[:PAD] + r[PAD:] + dot(bs[:PAD], low)
            f = acc[cell, i * PAD : (i + 1) * PAD, :] + r
            up = pltpu.roll(pltpu.roll(f, depth - 1, 1), 4, 0)
            down = pltpu.roll(pltpu.roll(f, 1, 1), PAD - 4, 0)
            f = f + jnp.where(take_up, up, 0.0) + jnp.where(take_down, down, 0.0)
            acc[cell, i * PAD : (i + 1) * PAD, :] = f
        return carry

    lax.fori_loop(0, cells, stiff, 0)

    def join(a, ra, b, rb, size):
        total = acc[a, ra : ra + size, :] + acc[b, rb : rb + size, :]
        acc[a, ra : ra + size, :] = total
        acc[b, rb : rb + size, :] = total

    for c in range(3):
        o = c * PAD
        for y in range(cy):
            for x in range(cx - 1):
                join(x * cy + y, o + 100, (x + 1) * cy + y, o, 25)
        for x in range(cx):
            for y in range(cy - 1):
                for p in range(5):
                    join(x * cy + y, o + p * 25 + 20, x * cy + y + 1, o + p * 25, 5)
        for y in range(cy):
            xs[0, y, c] = acc[y, o : o + 25, :]
            xs[1, y, c] = acc[(cx - 1) * cy + y, o + 100 : o + 125, :]
        for x in range(cx):
            for p in range(5):
                k = o + p * 25
                ys[0, x, c, p * 5 : p * 5 + 5, :] = acc[x * cy, k : k + 5, :]
                ys[1, x, c, p * 5 : p * 5 + 5, :] = acc[x * cy + cy - 1, k + 20 : k + 25, :]
        for x in range(2):
            for y in range(2):
                cell = x * (cx - 1) * cy + y * (cy - 1)
                k = o + x * 100 + y * 20
                cs[x, y, c] = acc[cell, k : k + 5, :]
        for cell in range(cells):
            out[cell, c] = acc[cell, o : o + 125, :]


def halo_kernel(nx, ny, xs, ys, cs, rx, ry, rc, send_sem, recv_sem):
    gx, gy = lax.axis_index("gx"), lax.axis_index("gy")
    moves = []
    for side in (0, 1):
        moves.append((2 * side - 1, 0, xs.at[side], rx.at[1 - side], rx.at[side]))
    for side in (0, 1):
        moves.append((0, 2 * side - 1, ys.at[side], ry.at[1 - side], ry.at[side]))
    for x in (0, 1):
        for y in (0, 1):
            moves.append((2 * x - 1, 2 * y - 1, cs.at[x, y], rc.at[1 - x, 1 - y], rc.at[x, y]))
    opposite = [1, 0, 3, 2, 7, 6, 5, 4]
    barrier = pltpu.get_barrier_semaphore()

    def there(dx, dy):
        ok = None
        for pos, step, count in ((gx, dx, nx), (gy, dy, ny)):
            if step:
                c = pos > 0 if step < 0 else pos < count - 1
                ok = c if ok is None else ok & c
        return ok

    waits = jnp.int32(0)
    for dx, dy, src, dst, mine in moves:
        @pl.when(there(dx, dy))
        def _():
            pl.semaphore_signal(barrier, inc=1, device_id=(gx + dx, gy + dy), device_id_type=MESH)

        waits = waits + there(dx, dy).astype(jnp.int32)
    pl.semaphore_wait(barrier, waits)

    def copy(m, at, landing):
        dx, dy, src, dst, mine = moves[m]
        return pltpu.make_async_remote_copy(
            src_ref=src,
            dst_ref=landing,
            send_sem=send_sem.at[m],
            recv_sem=recv_sem.at[at],
            device_id=(gx + dx, gy + dy),
            device_id_type=MESH,
        )

    for m, (dx, dy, src, dst, mine) in enumerate(moves):
        @pl.when(there(dx, dy))
        def _():
            copy(m, m, dst).start()

        @pl.when(jnp.logical_not(there(dx, dy)))
        def _():
            mine[...] = jnp.zeros_like(mine)

    for m, (dx, dy, src, dst, mine) in enumerate(moves):
        @pl.when(there(dx, dy))
        def _():
            copy(m, opposite[m], mine).wait_recv()
            copy(m, m, dst).wait_send()


def join_kernel(cx, cy, field, rx, ry, rc, out):
    out[...] = field[...]
    for c in range(3):
        for y in range(cy):
            out[y, c, 0:25, :] += rx[0, y, c]
            out[(cx - 1) * cy + y, c, 100:125, :] += rx[1, y, c]
        for x in range(cx):
            for p in range(5):
                k = p * 25
                out[x * cy, c, k : k + 5, :] += ry[0, x, c, p * 5 : p * 5 + 5, :]
                out[x * cy + cy - 1, c, k + 20 : k + 25, :] += ry[1, x, c, p * 5 : p * 5 + 5, :]
        for x in range(2):
            for y in range(2):
                cell = x * (cx - 1) * cy + y * (cy - 1)
                k = x * 100 + y * 20
                out[cell, c, k : k + 5, :] += rc[x, y, c]


def vmem(count):
    return [pl.BlockSpec(memory_space=pltpu.VMEM)] * count


def body(nx, ny, wavefield, moduli, residuals, coords, angles, element_ids, counts):
    cx, cy, depth = wavefield.shape[0], wavefield.shape[1], wavefield.shape[4]
    n, slots = nx * ny, residuals.shape[2]
    cells = cx * cy
    shape = jax.ShapeDtypeStruct
    recv = pl.pallas_call(
        functools.partial(scatter_kernel, nx, ny),
        out_shape=shape((n, 8, slots), F32),
        in_specs=vmem(5),
        out_specs=vmem(1)[0],
        scratch_shapes=[
            pltpu.VMEM((n, 8, slots), F32),
            pltpu.VMEM((n, 8, slots), F32),
            pltpu.SemaphoreType.DMA((n,)),
            pltpu.SemaphoreType.DMA((n,)),
        ],
        compiler_params=pltpu.CompilerParams(collective_id=0, has_side_effects=True),
    )(residuals, coords, angles, element_ids, counts)
    strips = (
        shape((2, cy, 3, 25, depth), F32),
        shape((2, cx, 3, 25, depth), F32),
        shape((2, 2, 3, 5, depth), F32),
    )
    field, xs, ys, cs = pl.pallas_call(
        functools.partial(force_kernel, cx, cy),
        out_shape=(shape((cells, 3, 125, depth), F32),) + strips,
        in_specs=vmem(8),
        out_specs=tuple(vmem(4)),
        scratch_shapes=[
            pltpu.VMEM((cells, 3 * PAD, depth), F32),
            pltpu.VMEM((6 * PAD, GROUP * slots), BF16),
            pltpu.VMEM((cells * depth, GROUP * slots), BF16),
            pltpu.VMEM((PAD, depth), F32),
        ],
    )(
        wavefield.reshape(cells, 3, 125, depth),
        moduli.reshape(cells, 2, depth),
        recv,
        *tables(),
    )
    rx, ry, rc = pl.pallas_call(
        functools.partial(halo_kernel, nx, ny),
        out_shape=strips,
        in_specs=vmem(3),
        out_specs=tuple(vmem(3)),
        scratch_shapes=[pltpu.SemaphoreType.DMA((8,)), pltpu.SemaphoreType.DMA((8,))],
        compiler_params=pltpu.CompilerParams(collective_id=1, has_side_effects=True),
    )(xs, ys, cs)
    force = pl.pallas_call(
        functools.partial(join_kernel, cx, cy),
        out_shape=shape((cells, 3, 125, depth), F32),
        in_specs=vmem(4),
        out_specs=vmem(1)[0],
    )(field, rx, ry, rc)
    return force.reshape(cx, cy, 3, 125, depth)


def solution(mesh):
    in_specs = (
        P("gx", "gy", None, None, None),
        P("gx", "gy", None, None),
        P(("gx", "gy"), None, None),
        P(("gx", "gy"), None, None, None),
        P(("gx", "gy"), None, None, None),
        P(("gx", "gy"), None, None),
        P(("gx", "gy"), None),
    )
    out_specs = P("gx", "gy", None, None, None)
    return jax.shard_map(
        functools.partial(body, mesh.shape["gx"], mesh.shape["gy"]),
        mesh=mesh,
        in_specs=in_specs,
        out_specs=out_specs,
        check_vma=False,
    )
```

time: 155 us -> 57.8 us (0.37)
  the two profiles are of different devices: /device:TPU:9 before, /device:TPU:0 now
where the time goes in v1:
time: 57.8 us; the launch traced here: 57.5 us
  Pallas kernels  49.6 us (86%)
  local copies, waits for them, and re-layouts  7.89 us (14%)
    pallas_call x1, Pallas kernels, body(): pl.pallas_call(functools.partial(force_kernel, cx, cy), out_shape=(shape(...  18.4 us
    pallas_call x1, Pallas kernels, body(): pl.pallas_call(functools.partial(halo_kernel, nx, ny), out_shape=strips,...  14.5 us
    pallas_call x1, Pallas kernels, body(): pl.pallas_call(functools.partial(scatter_kernel, nx, ny), out_shape=shape...  13.6 us
    unnamed x2, local copies, waits for them, and re-layouts  4.17 us
    reshape x1, local copies, waits for them, and re-layouts, body(): return force.reshape(cx, cy, 3, 125, depth)  3.72 us
    pallas_call x1, Pallas kernels, body(): pl.pallas_call(functools.partial(join_kernel, cx, cy), out_shape=shape((c...  3.03 us

profile of v1, /device:TPU:0, one launch (start us, length us, event | category | flops | bytes accessed | tf_op | source)
XLA Modules:
  0.0 57.5 jit_solution(13104433359021553623)
XLA Ops:
  0.0 1.5 %copy.14.coord = f32[1,32,3,128]{3,2,1,0:T(4,128)} copy(f32[1,32,3,128]{3,1,2,0:T(8,128)} %param.15) | data formatting | bytes 98304 | tf_op args[3]
  1.5 13.6 %shard_map.118.recv = f32[32,8,128]{2,1,0:T(8,128)} custom-call(f32[1,32,128]{2,1,0:T(8,128)} %resid.1, f32[1,32,3,128]{3,2,1,0:T(4,128)} %copy.14.coord, f32[1,32,2,128]{3,2,1,0:T(2,128)} %angle.1, s32[1,32,128]{2,1,0:T(8,128)} %ids.1, s32[1,32]{1,0:T(1,128)} %count.1), custom_call_target="tpu_custom_call" | custom-call | tf_op jit(solution)/shard_map/pallas_call | solution.py:372
  15.0 2.7 %copy.13 = f32[2,2,3,125,256]{4,3,2,1,0:T(8,128)} copy(f32[2,2,3,125,256]{4,1,3,2,0:T(2,128)} %param.12) | data formatting | bytes 3072000 | tf_op args[0]
  17.7 18.4 %shard_map.119 = (f32[4,3,125,256]{3,2,1,0:T(8,128)}, f32[2,2,3,25,256]{4,3,2,1,0:T(8,128)}, f32[2,2,3,25,256]{4,3,2,1,0:T(8,128)}, f32[2,2,3,5,256]{4,3,2,1,0:T(8,128)}) custom-call(f32[4,3,125,256]{3,2,1,0:T(8,128)} %bitcast.3, f32[4,2,256]{2,1,0:T(2,128)} %bitcast.5, f32[32,8,128]{2,1,0:T(8,128)} %shard_map.118.recv, bf16[384,256]{1,0:T(8,128)(2,1)} %constant.10.clone.g1, ...), custom_call_target="tpu_custom_call" | custom-call | tf_op jit(solution)/shard_map/pallas_call | solution.py:390
  36.2 14.5 %shard_map.120 = (f32[2,2,3,25,256]{4,3,2,1,0:T(8,128)}, f32[2,2,3,25,256]{4,3,2,1,0:T(8,128)}, f32[2,2,3,5,256]{4,3,2,1,0:T(8,128)}) custom-call(f32[2,2,3,25,256]{4,3,2,1,0:T(8,128)} %get-tuple-element.13.xs, f32[2,2,3,25,256]{4,3,2,1,0:T(8,128)} %get-tuple-element.14.ys, f32[2,2,3,5,256]{4,3,2,1,0:T(8,128)} %get-tuple-element.15.cs), custom_call_target="tpu_custom_call" | custom-call | tf_op jit(solution)/shard_map/pallas_call | solution.py:407
  50.7 3.0 %shard_map.121 = f32[4,3,125,256]{3,2,1,0:T(8,128)} custom-call(f32[4,3,125,256]{3,2,1,0:T(8,128)} %get-tuple-element.12.field, f32[2,2,3,25,256]{4,3,2,1,0:T(8,128)} %get-tuple-element.16.rx, f32[2,2,3,25,256]{4,3,2,1,0:T(8,128)} %get-tuple-element.17.ry, f32[2,2,3,5,256]{4,3,2,1,0:T(8,128)} %get-tuple-element.18.rc), custom_call_target="tpu_custom_call" | custom-call | tf_op jit(solution)/shard_map/pallas_call | solution.py:415
  53.7 3.7 %copy.15 = f32[2,2,3,125,256]{4,1,3,2,0:T(2,128)} copy(f32[2,2,3,125,256]{4,3,2,1,0:T(8,128)} %bitcast.4) | data formatting | bytes 3072000 | tf_op jit(solution)/shard_map/reshape | solution.py:421

commit v2 on v1

v2 whole, which is shorter than its diff:
```python
import functools
import math

import jax
import jax.numpy as jnp
import numpy as np
from jax import lax
from jax.experimental import pallas as pl
from jax.experimental.pallas import tpu as pltpu
from jax.sharding import PartitionSpec as P

MESH = pl.DeviceIdType.MESH
F32, BF16 = jnp.float32, jnp.bfloat16
PAD = 128
SPAN = 32


def gll_points():
    return np.array([-1.0, -math.sqrt(3.0 / 7.0), 0.0, math.sqrt(3.0 / 7.0), 1.0])


def gll_weights():
    return np.array([0.1, 49.0 / 90.0, 32.0 / 45.0, 49.0 / 90.0, 0.1])


def derivative_table():
    points = gll_points()
    table = np.zeros((5, 5))
    for row in range(5):
        for col in range(5):
            if row == col:
                table[row, col] = sum(
                    (1.0 / (points[col] - points[other]) for other in range(5) if other != col)
                )
            else:
                value = 1.0 / (points[col] - points[row])
                for other in range(5):
                    if other != col and other != row:
                        value = (
                            value * (points[row] - points[other]) / (points[col] - points[other])
                        )
                table[row, col] = value
    return table


def split_table(table):
    high = table.astype(BF16)
    return high, (table - high.astype(np.float64)).astype(BF16)


def tables():
    dm, eye = derivative_table(), np.eye(5)
    w1 = gll_weights()
    weight = (w1[:, None, None] * w1[None, :, None] * w1[None, None, :]).reshape(-1)
    dirs = [
        np.kron(np.kron(dm, eye), eye),
        np.kron(np.kron(eye, dm), eye),
        np.kron(np.kron(eye, eye), dm),
    ]
    grad = np.zeros((3 * PAD, PAD))
    back = np.zeros((PAD, 3 * PAD))
    for j in range(3):
        grad[j * PAD : j * PAD + 125, :125] = dirs[j]
        back[:125, j * PAD : j * PAD + 125] = -dirs[j].T * weight[None, :]
    gh, gl = split_table(grad)
    bh, bl = split_table(back)
    g1 = np.concatenate([gh, gh], 1)
    bs = np.concatenate([bh, bl], 0)
    spread = np.zeros((4 * PAD, 192))
    for p in range(5):
        for q in range(5):
            for r in range(5):
                n = (p * 5 + q) * 5 + r
                for base, col in ((0, p * 8 + q), (1, 40 + p * 8 + q), (2, 80 + r), (3, 88 + r)):
                    spread[base * PAD + n, col] = 1.0
                    spread[base * PAD + n, 96 + col] = 1.0
    points = gll_points()
    consts = np.zeros((8, 8, 128), np.float32)
    for q in range(5):
        others = [k for k in range(5) if k != q]
        for j, k in enumerate(others):
            consts[j, q] = points[k]
            consts[4 + j, q] = 1.0 / (points[q] - points[k])
    return (
        jnp.asarray(g1),
        jnp.asarray(gl),
        jnp.asarray(bs),
        jnp.asarray(spread.astype(BF16)),
        jnp.asarray(consts),
    )


def split(x):
    high = x.astype(BF16)
    return high, (x - high.astype(F32)).astype(BF16)


def dot(a, b):
    return jnp.dot(a, b, preferred_element_type=F32)


def dot_t(a, b):
    return lax.dot_general(a, b, (((1,), (1,)), ((), ())), preferred_element_type=F32)


def basis(row, const):
    x = jnp.broadcast_to(row, const[0].shape)
    value = slope = None
    for j in range(4):
        scale = const[4 + j]
        factor = (x - const[j]) * scale
        if value is None:
            value, slope = factor, scale
        else:
            slope = slope * factor + value * scale
            value = value * factor
    return value, slope


def step_kernel(
    nx, ny, cx, cy, resid, coord, angle, ids, count, u_ref, mod_ref, g1, g2, bs, spread, consts,
    out, packed, got, acc, lhs, hot, pad, xs, ys, cs, rx, ry, rc,
    send_sem, recv_sem, halo_send, halo_recv,
):
    n = nx * ny
    gx, gy = lax.axis_index("gx"), lax.axis_index("gy")
    me = gx * ny + gy
    cells, depth, slots = cx * cy, acc.shape[2], resid.shape[2]
    halves = depth // 128
    rows_node = halves * cy
    span = min(n, SPAN)
    width = 2 * slots
    barrier = pltpu.get_barrier_semaphore()

    def greet(k, c):
        to = lax.rem(me + k, n)
        pl.semaphore_signal(
            barrier, inc=1, device_id=(to // ny, lax.rem(to, ny)), device_id_type=MESH
        )
        return c

    lax.fori_loop(1, n, greet, 0)
    rows = lax.broadcasted_iota(jnp.int32, (n, n), 0)
    cols = lax.broadcasted_iota(jnp.int32, (n, n), 1)
    diagonal = jnp.where(rows == cols, count[...].astype(F32), 0.0)
    live_count = jnp.sum(diagonal, axis=1, keepdims=True)
    slot = lax.broadcasted_iota(jnp.int32, (n, slots), 1).astype(F32)
    az, dip = angle[0, :, 0, :], angle[0, :, 1, :]
    cd = jnp.cos(dip)
    packed[:, 0, :] = jnp.where(slot < live_count, resid[0], 0.0)
    for d in range(3):
        packed[:, 1 + d, :] = coord[0, d]
    packed[:, 4, :] = jnp.cos(az) * cd
    packed[:, 5, :] = jnp.sin(az) * cd
    packed[:, 6, :] = jnp.sin(dip)
    packed[:, 7, :] = ids[0].astype(F32)
    pl.semaphore_wait(barrier, n - 1)

    def tile_copy(k, to, at):
        return pltpu.make_async_remote_copy(
            src_ref=packed.at[to],
            dst_ref=got.at[at],
            send_sem=send_sem.at[k],
            recv_sem=recv_sem.at[k],
            device_id=(to // ny, lax.rem(to, ny)),
            device_id_type=MESH,
        )

    def send(k, c):
        tile_copy(k, lax.rem(me + k, n), me).start()
        return c

    lax.fori_loop(1, n, send, 0)
    got[me] = packed[me]

    pad[...] = jnp.zeros_like(pad)

    def stiff(cell, carry):
        g = []
        for c in range(3):
            start = ((cell // cy) * 3 + c) * 125 * rows_node + lax.rem(cell, cy)
            for h in range(halves):
                pad[0:125, h * 128 : (h + 1) * 128] = u_ref[
                    pl.ds(start + h * cy, 125, stride=rows_node), :
                ]
            high, low = split(pad[...])
            r = dot(g1[...], jnp.concatenate([high, low], axis=0)) + dot(g2[...], high)
            g.append([r[j * PAD : (j + 1) * PAD] for j in range(3)])
        lam, mu = mod_ref[cell, 0:1, :], mod_ref[cell, 1:2, :]
        press = lam * (g[0][0] + g[1][1] + g[2][2])
        for i in range(3):
            parts = []
            for j in range(3):
                s = mu * (g[i][j] + g[j][i])
                parts.append(s + press if i == j else s)
            high, low = split(jnp.concatenate(parts, axis=0))
            r = dot(bs[...], high)
            acc[cell, i * PAD : (i + 1) * PAD, :] = r[:PAD] + r[PAD:] + dot(bs[:PAD], low)
        return carry

    lax.fori_loop(0, cells, stiff, 0)

    def arrive(k, c):
        tile_copy(k, lax.rem(me + k, n), lax.rem(me - k + n, n)).wait_recv()
        return c

    lax.fori_loop(1, n, arrive, 0)

    def prepare(first_tile):
        def pair(k, carry):
            at = first_tile + 2 * k
            tile = jnp.concatenate([got[at], got[at + 1]], axis=1)
            const = [jnp.concatenate([consts[j], consts[j]], axis=1) for j in range(8)]
            v = tile[0:1]
            t = [tile[4 + i : 5 + i] for i in range(3)]
            lx, dx = basis(tile[1:2], const)
            ly, dy = basis(tile[2:3], const)
            lz, dz = basis(tile[3:4], const)
            dx, dy, dz = dx * t[0], dy * t[1], dz * t[2]
            first = [dx[p : p + 1] * ly + lx[p : p + 1] * dy for p in range(5)]
            second = [lx[p : p + 1] * ly for p in range(5)]
            high, low = split(jnp.concatenate(first + second + [lz, dz], axis=0))
            wide = dot(spread[...], jnp.concatenate([high, low], axis=0))
            shape = wide[:PAD] * wide[2 * PAD : 3 * PAD] + wide[PAD : 2 * PAD] * wide[3 * PAD :]
            cols = pl.ds(pl.multiple_of(k * width, width), width)
            for i in range(3):
                high, low = split(shape * (v * t[i]))
                lhs[i, :PAD, cols] = high
                lhs[i, PAD:, cols] = low
            ident = tile[7:8].astype(jnp.int32)
            number = lax.broadcasted_iota(jnp.int32, (cells * depth, width), 0)
            hot[:, cols] = jnp.where(number == ident, 1.0, 0.0).astype(BF16)
            return carry

        lax.fori_loop(0, span // 2, pair, 0)

    def gather(i, cell):
        r = dot_t(lhs[i], hot[cell * depth : (cell + 1) * depth, :])
        return acc[cell, i * PAD : (i + 1) * PAD, :] + r[:PAD] + r[PAD:]

    if n > span:
        def early(b, carry):
            prepare(b * span)
            for i in range(3):
                for cell in range(cells):
                    acc[cell, i * PAD : (i + 1) * PAD, :] = gather(i, cell)
            return carry

        lax.fori_loop(0, n // span - 1, early, 0)
    prepare(n - span)

    node = lax.broadcasted_iota(jnp.int32, (PAD, depth), 0)
    lane = lax.broadcasted_iota(jnp.int32, (PAD, depth), 1)
    along = lax.rem(node, 5)
    take_up = (along == 4) & (lane < depth - 1)
    take_down = (along == 0) & (lane > 0)

    def join(a, ra, b, rb, size):
        total = acc[a, ra : ra + size, :] + acc[b, rb : rb + size, :]
        acc[a, ra : ra + size, :] = total
        acc[b, rb : rb + size, :] = total

    moves = []
    for side in (0, 1):
        moves.append((2 * side - 1, 0, xs, rx, (side,), (1 - side,)))
    for side in (0, 1):
        moves.append((0, 2 * side - 1, ys, ry, (side,), (1 - side,)))
    for x in (0, 1):
        for y in (0, 1):
            moves.append((2 * x - 1, 2 * y - 1, cs, rc, (x, y), (1 - x, 1 - y)))
    opposite = [1, 0, 3, 2, 7, 6, 5, 4]

    def there(m):
        ok = None
        for pos, step, total in ((gx, moves[m][0], nx), (gy, moves[m][1], ny)):
            if step:
                c = pos > 0 if step < 0 else pos < total - 1
                ok = c if ok is None else ok & c
        return ok

    def strip_copy(c, m, sem, place):
        dx, dy, src, dst, mine, theirs = moves[m]
        return pltpu.make_async_remote_copy(
            src_ref=src.at[(c,) + mine],
            dst_ref=dst.at[(c,) + place],
            send_sem=halo_send.at[c * 8 + m],
            recv_sem=halo_recv.at[c * 8 + sem],
            device_id=(gx + dx, gy + dy),
            device_id_type=MESH,
        )

    for m in range(8):
        @pl.when(jnp.logical_not(there(m)))
        def _():
            dst, mine = moves[m][3], moves[m][4]
            for c in range(3):
                hole = dst.at[(c,) + mine]
                hole[...] = jnp.zeros(hole.shape, F32)

    for c in range(3):
        o = c * PAD
        for cell in range(cells):
            f = gather(c, cell)
            up = pltpu.roll(pltpu.roll(f, depth - 1, 1), 4, 0)
            down = pltpu.roll(pltpu.roll(f, 1, 1), PAD - 4, 0)
            acc[cell, o : o + PAD, :] = (
                f + jnp.where(take_up, up, 0.0) + jnp.where(take_down, down, 0.0)
            )
        for y in range(cy):
            for x in range(cx - 1):
                join(x * cy + y, o + 100, (x + 1) * cy + y, o, 25)
        for x in range(cx):
            for y in range(cy - 1):
                for p in range(5):
                    join(x * cy + y, o + p * 25 + 20, x * cy + y + 1, o + p * 25, 5)
        for y in range(cy):
            xs[c, 0, y] = acc[y, o : o + 25, :]
            xs[c, 1, y] = acc[(cx - 1) * cy + y, o + 100 : o + 125, :]
        for x in range(cx):
            for p in range(5):
                k = o + p * 25
                ys[c, 0, x, p * 5 : p * 5 + 5, :] = acc[x * cy, k : k + 5, :]
                ys[c, 1, x, p * 5 : p * 5 + 5, :] = acc[x * cy + cy - 1, k + 20 : k + 25, :]
        for x in range(2):
            for y in range(2):
                cell = x * (cx - 1) * cy + y * (cy - 1)
                k = o + x * 100 + y * 20
                cs[c, x, y] = acc[cell, k : k + 5, :]
        for m in range(8):
            @pl.when(there(m))
            def _():
                strip_copy(c, m, m, moves[m][5]).start()

    def drain(k, c):
        tile_copy(k, lax.rem(me + k, n), me).wait_send()
        return c

    lax.fori_loop(1, n, drain, 0)

    for c in range(3):
        o = c * PAD
        for m in range(8):
            @pl.when(there(m))
            def _():
                strip_copy(c, m, opposite[m], moves[m][4]).wait_recv()
                strip_copy(c, m, m, moves[m][5]).wait_send()

        for y in range(cy):
            acc[y, o : o + 25, :] += rx[c, 0, y]
            acc[(cx - 1) * cy + y, o + 100 : o + 125, :] += rx[c, 1, y]
        for x in range(cx):
            for p in range(5):
                k = o + p * 25
                acc[x * cy, k : k + 5, :] += ry[c, 0, x, p * 5 : p * 5 + 5, :]
                acc[x * cy + cy - 1, k + 20 : k + 25, :] += ry[c, 1, x, p * 5 : p * 5 + 5, :]
        for x in range(2):
            for y in range(2):
                cell = x * (cx - 1) * cy + y * (cy - 1)
                k = o + x * 100 + y * 20
                acc[cell, k : k + 5, :] += rc[c, x, y]
        for cell in range(cells):
            start = ((cell // cy) * 3 + c) * 125 * rows_node + cell % cy
            for h in range(halves):
                out[pl.ds(start + h * cy, 125, stride=rows_node), :] = acc[
                    cell, o : o + 125, h * 128 : (h + 1) * 128
                ]


def vmem(count):
    return [pl.BlockSpec(memory_space=pltpu.VMEM)] * count


def body(nx, ny, wavefield, moduli, residuals, coords, angles, element_ids, counts):
    cx, cy, depth = wavefield.shape[0], wavefield.shape[1], wavefield.shape[4]
    n, slots = nx * ny, residuals.shape[2]
    cells, halves = cx * cy, depth // 128
    span = min(n, SPAN)
    rows = wavefield.transpose(0, 2, 3, 1, 4).reshape(cx, 3, 125, cy, halves, 128)
    rows = rows.transpose(0, 1, 2, 4, 3, 5).reshape(-1, 128)
    scratch = [
        pltpu.VMEM((n, 8, slots), F32),
        pltpu.VMEM((n, 8, slots), F32),
        pltpu.VMEM((cells, 3 * PAD, depth), F32),
        pltpu.VMEM((3, 2 * PAD, span * slots), BF16),
        pltpu.VMEM((cells * depth, span * slots), BF16),
        pltpu.VMEM((PAD, depth), F32),
    ]
    for _ in range(2):
        scratch += [
            pltpu.VMEM((3, 2, cy, 25, depth), F32),
            pltpu.VMEM((3, 2, cx, 25, depth), F32),
            pltpu.VMEM((3, 2, 2, 5, depth), F32),
        ]
    scratch += [
        pltpu.SemaphoreType.DMA((n,)),
        pltpu.SemaphoreType.DMA((n,)),
        pltpu.SemaphoreType.DMA((24,)),
        pltpu.SemaphoreType.DMA((24,)),
    ]
    force = pl.pallas_call(
        functools.partial(step_kernel, nx, ny, cx, cy),
        out_shape=jax.ShapeDtypeStruct(rows.shape, F32),
        in_specs=vmem(12),
        out_specs=vmem(1)[0],
        scratch_shapes=scratch,
        compiler_params=pltpu.CompilerParams(collective_id=0, has_side_effects=True),
    )(
        residuals,
        coords.transpose(0, 2, 1, 3),
        angles,
        element_ids,
        counts,
        rows,
        moduli.reshape(cells, 2, depth),
        *tables(),
    )
    force = force.reshape(cx, 3, 125, halves, cy, 128).transpose(0, 1, 2, 4, 3, 5)
    return force.reshape(cx, 3, 125, cy, depth).transpose(0, 3, 1, 2, 4)


def solution(mesh):
    in_specs = (
        P("gx", "gy", None, None, None),
        P("gx", "gy", None, None),
        P(("gx", "gy"), None, None),
        P(("gx", "gy"), None, None, None),
        P(("gx", "gy"), None, None, None),
        P(("gx", "gy"), None, None),
        P(("gx", "gy"), None),
    )
    out_specs = P("gx", "gy", None, None, None)
    return jax.shard_map(
        functools.partial(body, mesh.shape["gx"], mesh.shape["gy"]),
        mesh=mesh,
        in_specs=in_specs,
        out_specs=out_specs,
        check_vma=False,
    )
```

time: 57.8 us -> 42.2 us (0.73)
  Pallas kernels: 49.6 us -> 39 us
  local copies, waits for them, and re-layouts: 7.89 us -> 3.05 us
    pallas_call x4 -> x1, Pallas kernels: 49.6 us -> 39 us  [body(): pl.pallas_call(functools.partial(step_kernel, nx, ny, cx, cy), out_shape=...]
    reshape x1 -> x0, local copies, waits for them, and re-layouts: 3.72 us -> none  [body(): return force.reshape(cx, cy, 3, 125, depth)]
    unnamed x2 -> x1, local copies, waits for them, and re-layouts: 4.17 us -> 3.05 us
where the time goes in v2:
time: 42.2 us; the launch traced here: 42 us
  Pallas kernels  39 us (92%)
  local copies, waits for them, and re-layouts  3.05 us (7%)
    pallas_call x1, Pallas kernels, body(): pl.pallas_call(functools.partial(step_kernel, nx, ny, cx, cy), out_shape=...  39 us
    unnamed x1, local copies, waits for them, and re-layouts  3.05 us

profile of v2, /device:TPU:0, one launch (start us, length us, event | category | flops | bytes accessed | tf_op | source)
XLA Modules:
  0.0 42.0 jit_solution(3110975555915151102)
XLA Ops:
  0.0 39.0 %shard_map.118 = f32[3000,128]{1,0:T(8,128)} custom-call(f32[1,32,128]{2,1,0:T(8,128)} %resid.1, f32[1,3,32,128]{3,2,1,0:T(8,128)} %bitcast.18, f32[1,32,2,128]{3,2,1,0:T(2,128)} %angle.1, s32[1,32,128]{2,1,0:T(8,128)} %ids.1, s32[1,32]{1,0:T(1,128)} %count.1, f32[3000,128]{1,0:T(8,128)} %bitcast.17, f32[4,2,256]{2,1,0:T(2,128)} %bitcast.19, ...), custom_call_target="tpu_custom_call" | custom-call | tf_op jit(solution)/shard_map/pallas_call | solution.py:400
  39.0 3.1 %copy.15 = f32[2,2,3,125,256]{4,1,3,2,0:T(2,128)} copy(f32[2,2,3,125,256]{4,1,3,2,0:T(2,128)} %bitcast.16) | data formatting | bytes 3072000

commit v3 on v2

--- a/solution.py
+++ b/solution.py
@@ -154,25 +154,6 @@
     packed[:, 5, :] = jnp.sin(az) * cd
     packed[:, 6, :] = jnp.sin(dip)
     packed[:, 7, :] = ids[0].astype(F32)
-    pl.semaphore_wait(barrier, n - 1)
-
-    def tile_copy(k, to, at):
-        return pltpu.make_async_remote_copy(
-            src_ref=packed.at[to],
-            dst_ref=got.at[at],
-            send_sem=send_sem.at[k],
-            recv_sem=recv_sem.at[k],
-            device_id=(to // ny, lax.rem(to, ny)),
-            device_id_type=MESH,
-        )
-
-    def send(k, c):
-        tile_copy(k, lax.rem(me + k, n), me).start()
-        return c
-
-    lax.fori_loop(1, n, send, 0)
-    got[me] = packed[me]
-
     pad[...] = jnp.zeros_like(pad)
 
     def stiff(cell, carry):
@@ -198,7 +179,27 @@
             acc[cell, i * PAD : (i + 1) * PAD, :] = r[:PAD] + r[PAD:] + dot(bs[:PAD], low)
         return carry
 
-    lax.fori_loop(0, cells, stiff, 0)
+    lax.fori_loop(0, cells // 2, stiff, 0)
+    pl.semaphore_wait(barrier, n - 1)
+
+    def tile_copy(k, to, at):
+        return pltpu.make_async_remote_copy(
+            src_ref=packed.at[to],
+            dst_ref=got.at[at],
+            send_sem=send_sem.at[k],
+            recv_sem=recv_sem.at[k],
+            device_id=(to // ny, lax.rem(to, ny)),
+            device_id_type=MESH,
+        )
+
+    def send(k, c):
+        tile_copy(k, lax.rem(me + k, n), me).start()
+        return c
+
+    lax.fori_loop(1, n, send, 0)
+    got[me] = packed[me]
+
+    lax.fori_loop(cells // 2, cells, stiff, 0)
 
     def arrive(k, c):
         tile_copy(k, lax.rem(me + k, n), lax.rem(me - k + n, n)).wait_recv()

time: 42.2 us -> 42.3 us (level)
  no operation moved by 1% of the time
where the time goes in v3:
time: 42.3 us; the launch traced here: 42.1 us
  Pallas kernels  39.1 us (92%)
  local copies, waits for them, and re-layouts  3.05 us (7%)
    pallas_call x1, Pallas kernels, body(): pl.pallas_call(functools.partial(step_kernel, nx, ny, cx, cy), out_shape=...  39.1 us
    unnamed x1, local copies, waits for them, and re-layouts  3.05 us

profile of v3, /device:TPU:0, one launch (start us, length us, event | category | flops | bytes accessed | tf_op | source)
XLA Modules:
  0.0 42.1 jit_solution(17073930409757623510)
XLA Ops:
  0.0 39.1 %shard_map.118 = f32[3000,128]{1,0:T(8,128)} custom-call(f32[1,32,128]{2,1,0:T(8,128)} %resid.1, f32[1,3,32,128]{3,2,1,0:T(8,128)} %bitcast.18, f32[1,32,2,128]{3,2,1,0:T(2,128)} %angle.1, s32[1,32,128]{2,1,0:T(8,128)} %ids.1, s32[1,32]{1,0:T(1,128)} %count.1, f32[3000,128]{1,0:T(8,128)} %bitcast.17, f32[4,2,256]{2,1,0:T(2,128)} %bitcast.19, ...), custom_call_target="tpu_custom_call" | custom-call | tf_op jit(solution)/shard_map/pallas_call | solution.py:401
  39.1 3.1 %copy.15 = f32[2,2,3,125,256]{4,1,3,2,0:T(2,128)} copy(f32[2,2,3,125,256]{4,1,3,2,0:T(2,128)} %bitcast.16) | data formatting | bytes 3072000
